TPU v7x, 32 devices: a whole 2x2x4 slice. The times are simulated.
32 devices in a mesh: head: 4 (over z), outer: 2 (over core), inner: 4 (over y, x).
Axes of the slice: x: 2, y: 2, z: 4, core: 2. Of those that a mesh axis runs over, the one named last changes fastest.
Arguments:
- query: bfloat16 [4096, 8192], P(('outer', 'inner', 'head')), may hold values from -100 to 100
- keys: bfloat16 [4096, 1024], P(('outer', 'inner', 'head')), may hold values from -4.5 to 4.5
- values: bfloat16 [4096, 1024], P(('outer', 'inner', 'head')), may hold values from -6 to 6
- lengths: int32 [8], replicated, may hold values from 1 to 1024, 4096 in all
Outputs:
- attended: bfloat16 [4096, 8192], P(('outer', 'inner', 'head'))
Inputs may be any that keep to these rules, and one draw needn't show every extreme that they name: `lengths`: they sum to 4096, and the longest is exactly 1024.
All inputs are finite; a program needn't handle non-finite values.
Results may differ from a plain program's by a relative error of at most 0.0038.
Values may be sent and summed in bfloat16 or wider, within the bound.
A program may use at most 64 MiB of HBM per device.

v0:
```python
import math
import jax
import jax.numpy as jnp
from jax import lax
from jax.sharding import PartitionSpec as P

HEAD_SIZE = 128


def from_behind(value, axis, steps):
    count = lax.axis_size(axis)
    leading, last = (max(0, -steps), min(count, count - steps))
    return lax.ppermute(value, axis, [(source, source + steps) for source in range(leading, last)])


def doc_numbers(lengths, start_pos, count):
    ends = jnp.cumsum(lengths)
    positions = start_pos + lax.iota(jnp.int32, count)
    numbers = jnp.sum((positions[:, None] >= ends[None, :]).astype(jnp.int32), axis=1)
    return (numbers, positions)


def per_device(query, keys, values, lengths):
    query_local, keys_local, values_local = (
        lax.all_to_all(query, "head", split_axis=1, concat_axis=0, tiled=True),
        lax.all_to_all(keys, "head", split_axis=1, concat_axis=0, tiled=True),
        lax.all_to_all(values, "head", split_axis=1, concat_axis=0, tiled=True),
    )
    local_len = query_local.shape[0]
    pair_heads = keys_local.shape[1] // HEAD_SIZE
    group_width = query_local.shape[1] // keys_local.shape[1]
    context_count = lax.axis_size(("outer", "inner"))
    reach_hops = min(2, context_count // 4)
    position_index = lax.axis_index(("outer", "inner"))
    query_docs, query_pos = doc_numbers(lengths, position_index * local_len, local_len)
    query_groups = jnp.transpose(
        query_local.reshape(local_len, pair_heads, group_width, HEAD_SIZE), (2, 0, 1, 3)
    )
    score_scale = 1.0 / math.sqrt(HEAD_SIZE)

    def attend(state, stacked, distance):
        key_heads = stacked[0].reshape(local_len, pair_heads, HEAD_SIZE)
        value_heads = stacked[1].reshape(local_len, pair_heads, HEAD_SIZE)
        key_docs, key_pos = doc_numbers(lengths, (position_index - distance) * local_len, local_len)
        visible = (
            (query_docs[:, None] == key_docs[None, :])
            & (key_pos[None, :] <= query_pos[:, None])
            & (key_pos[None, :] >= 0)
        )

        def one_group(operands):
            query_part, running_max, running_total, running_sum = operands
            scores = (
                jnp.einsum(
                    "qkd,ckd->kqc", query_part, key_heads, preferred_element_type=jnp.float32
                )
                * score_scale
            )
            masked = jnp.where(visible, scores, -1e30)
            new_max = jnp.maximum(running_max, jnp.max(masked, axis=2))
            weights = jnp.where(visible, jnp.exp(masked - new_max[..., None]), 0.0)
            shrink = jnp.exp(running_max - new_max)
            new_total = running_total * shrink + jnp.sum(weights, axis=2)
            update = jnp.einsum(
                "kqc,ckd->qkd",
                weights.astype(jnp.bfloat16),
                value_heads,
                preferred_element_type=jnp.float32,
            )
            new_sum = running_sum * jnp.transpose(shrink, (1, 0))[..., None] + update
            return (new_max, new_total, new_sum)

        return lax.map(one_group, (query_groups, state[0], state[1], state[2]))

    start_state = (
        jnp.full((group_width, pair_heads, local_len), -1e30, jnp.float32),
        jnp.zeros((group_width, pair_heads, local_len), jnp.float32),
        jnp.zeros((group_width, local_len, pair_heads, HEAD_SIZE), jnp.float32),
    )
    own_pair = jnp.stack((keys_local, values_local))
    state = attend(start_state, own_pair, 0)
    carried = own_pair
    for distance in range(1, reach_hops + 1):
        carried = from_behind(carried, ("outer", "inner"), 1)
        state = attend(state, carried, distance)
    running_max, running_total, running_sum = state
    outcome = running_sum / jnp.transpose(running_total, (0, 2, 1))[..., None]
    outcome = jnp.transpose(outcome, (1, 2, 0, 3))
    outcome = outcome.reshape(local_len, pair_heads * group_width * HEAD_SIZE).astype(jnp.bfloat16)
    return lax.all_to_all(outcome, "head", split_axis=0, concat_axis=1, tiled=True)


def solution(mesh):
    placed = (
        P(("outer", "inner", "head"), None),
        P(("outer", "inner", "head"), None),
        P(("outer", "inner", "head"), None),
        P(),
    )
    return jax.shard_map(
        per_device,
        mesh=mesh,
        in_specs=placed,
        out_specs=P(("outer", "inner", "head"), None),
        check_vma=False,
    )
```

profile of v0, /device:TPU:0, one launch (start us, length us, event | category | flops | bytes accessed | tf_op | source)
XLA Modules:
  0.0 246.9 jit_solution(3934203246122695590)
XLA Ops:
  0.0 1.9 copy.56
  1.9 6.3 %all-to-all-start.1 = ((bf16[128,4,256]{0,2,1:T(8,128)(2,1)}), bf16[128,4,256]{0,2,1:T(8,128)(2,1)S(1)}, u32[]{:S(2)}, u32[]{:S(2)}) async-start(bf16[128,4,256]{0,2,1:T(8,128)(2,1)} %bitcast.2), calls=%async_computation.1 | async-start | bytes 524288 | tf_op jit(solution)/shard_map/all_to_all | solution.py:26
  8.3 1.8 copy.58
  10.1 7.1 %all-to-all-done.1 = bf16[128,4,256]{0,2,1:T(8,128)(2,1)S(1)} async-done(((bf16[128,4,256]{0,2,1:T(8,128)(2,1)}), bf16[128,4,256]{0,2,1:T(8,128)(2,1)S(1)}, u32[]{:S(2)}, u32[]{:S(2)}) %all-to-all-start.1) | async-done | bytes 262176 | tf_op jit(solution)/shard_map/all_to_all | solution.py:26
  17.2 3.4 %all-to-all-start.2 = ((bf16[128,4,256]{0,2,1:T(8,128)(2,1)}), bf16[128,4,256]{0,2,1:T(8,128)(2,1)S(1)}, u32[]{:S(2)}, u32[]{:S(2)}) async-start(bf16[128,4,256]{0,2,1:T(8,128)(2,1)} %bitcast.4), calls=%async_computation.2 | async-start | bytes 524288 | tf_op jit(solution)/shard_map/all_to_all | solution.py:27
  20.6 1.6 copy.84
  22.2 5.4 %all-to-all-done.2 = bf16[128,4,256]{0,2,1:T(8,128)(2,1)S(1)} async-done(((bf16[128,4,256]{0,2,1:T(8,128)(2,1)}), bf16[128,4,256]{0,2,1:T(8,128)(2,1)S(1)}, u32[]{:S(2)}, u32[]{:S(2)}) %all-to-all-start.2) | async-done | bytes 262176 | tf_op jit(solution)/shard_map/all_to_all | solution.py:27
  27.6 3.6 %all-to-all-start = ((bf16[128,4,2048]{2,0,1:T(8,128)(2,1)}), bf16[128,4,2048]{2,0,1:T(8,128)(2,1)S(1)}, u32[]{:S(2)}, u32[]{:S(2)}) async-start(bf16[128,4,2048]{2,0,1:T(8,128)(2,1)} %bitcast.143), calls=%async_computation | async-start | bytes 4194304 | tf_op jit(solution)/shard_map/all_to_all | solution.py:25
  31.6 4.2 %collective-permute-start = (bf16[2,512,256]{2,1,0:T(8,128)(2,1)S(1)}, bf16[2,512,256]{2,1,0:T(8,128)(2,1)}, u32[]{:S(2)}, u32[]{:S(2)}) collective-permute-start(bf16[2,512,256]{2,1,0:T(8,128)(2,1)S(1)} %pad_maximum_fusion), channel_id=1, source_target_pairs={{0,1},{1,2},{2,3},{3,4},{4,5},{5,6},{6,7},{8,9},{9,10},{10,11},{11... | collective-permute-start | bytes 1572872 | tf_op jit(solution)/shard_map/ppermute | solution.py:13
  35.8 7.3 %collective-permute-done = bf16[2,512,256]{2,1,0:T(8,128)(2,1)} collective-permute-done((bf16[2,512,256]{2,1,0:T(8,128)(2,1)S(1)}, bf16[2,512,256]{2,1,0:T(8,128)(2,1)}, u32[]{:S(2)}, u32[]{:S(2)}) %collective-permute-start) | collective-permute-done | bytes 524320 | tf_op jit(solution)/shard_map/ppermute | solution.py:13
  43.2 5.3 %collective-permute-start.1 = (bf16[2,512,256]{2,1,0:T(8,128)(2,1)}, bf16[2,512,256]{2,1,0:T(8,128)(2,1)}, u32[]{:S(2)}, u32[]{:S(2)}) collective-permute-start(bf16[2,512,256]{2,1,0:T(8,128)(2,1)} %collective-permute-done), channel_id=1, source_target_pairs={{0,1},{1,2},{2,3},{3,4},{4,5},{5,6},{6,7},{8,9},{9,10},{10,11},{11... | collective-permute-start | bytes 1572872 | tf_op jit(solution)/shard_map/ppermute | solution.py:13
  48.9 0.8 copy.62
  49.7 1.1 fusion.75
  51.2 0.8 copy.69
  52.1 5.0 %collective-permute-done.1 = bf16[2,512,256]{2,1,0:T(8,128)(2,1)} collective-permute-done((bf16[2,512,256]{2,1,0:T(8,128)(2,1)}, bf16[2,512,256]{2,1,0:T(8,128)(2,1)}, u32[]{:S(2)}, u32[]{:S(2)}) %collective-permute-start.1) | collective-permute-done | bytes 524320 | tf_op jit(solution)/shard_map/ppermute | solution.py:13
  57.1 1.1 fusion.74
  58.8 17.9 %all-to-all-done = bf16[128,4,2048]{2,0,1:T(8,128)(2,1)S(1)} async-done(((bf16[128,4,2048]{2,0,1:T(8,128)(2,1)}), bf16[128,4,2048]{2,0,1:T(8,128)(2,1)S(1)}, u32[]{:S(2)}, u32[]{:S(2)}) %all-to-all-start) | async-done | bytes 2097184 | tf_op jit(solution)/shard_map/all_to_all | solution.py:25
  76.7 0.6 copy.82
  77.8 2.4 broadcast.125.clone.1
  80.3 27.0 %while.43 = (s32[]{:T(128)}, f32[8,2,512]{2,1,0:T(2,128)S(1)}, f32[8,2,512]{2,1,0:T(2,128)S(1)}, f32[8,512,2,128]{3,1,2,0:T(8,128)}, bf16[8,512,2,128]{3,1,2,0:T...) while((s32[]{:T(128)}, f32[8,2,512]{2,1,0:T(2,128)S(1)}, ...), condition=%wide.region_5.6_spmd.clone, body=%wide.region_2.0_spmd.clone.sunk | while | flops 276435968 | bytes 9753745 | solution.py:73
  81.4 1.8 fusion.111
  83.2 0.6 fusion.109
  84.7 1.8 fusion.111
  86.6 0.6 fusion.109
  88.1 1.8 fusion.111
  89.9 0.6 fusion.109
  91.5 1.8 fusion.111
  93.2 0.6 fusion.109
  94.8 1.8 fusion.111
  96.6 0.6 fusion.109
  98.2 1.8 fusion.111
  100.0 0.6 fusion.109
  101.5 1.8 fusion.111
  103.3 0.6 fusion.109
  104.8 1.8 fusion.111
  106.6 0.6 fusion.109
  107.2 2.4 broadcast.125.clone
  109.6 34.8 %while.44 = (s32[]{:T(128)}, f32[8,2,512]{2,1,0:T(2,128)S(1)}, f32[8,2,512]{2,1,0:T(2,128)S(1)}, f32[8,512,2,128]{3,1,2,0:T(8,128)}, f32[8,2,512]{2,1,0:T(2,128)...) while((s32[]{:T(128)}, f32[8,2,512]{2,1,0:T(2,128)S(1)}, ...), condition=%wide.region_10.11_spmd.clone, body=%wide.region_7.10_spmd.clone.sunk | while | flops 276566016 | bytes 9245857 | solution.py:73
  110.6 2.8 %fusion.119 = f32[8,512,2,128]{3,1,2,0:T(8,128)} fusion(f32[8,512,2,128]{3,1,2,0:T(8,128)} %get-tuple-element.807, s32[]{:T(128)} %get-tuple-element.804, bf16[512,2,128]{2,0,1:T(8,128)(2,1)S(1)} %get-tuple-element.829, f32[2,512,512]{1,2,0:T(8,128)S(1)} %get-tuple-element.731, f32[2,512]{1,0:T(2,128)S(1)} %get-tuple-element.733, ...), kind=kOutput, calls=%fused_computation.40.clone.1 | convolution fusion | flops 137101312 | bytes 3678720 | tf_op jit(solution)/shard_map/while/body/eval_jaxpr/kqc,ckd->qkd/dot_general | solution.py:64
  114.9 2.8 %fusion.119 = f32[8,512,2,128]{3,1,2,0:T(8,128)} fusion(f32[8,512,2,128]{3,1,2,0:T(8,128)} %get-tuple-element.807, s32[]{:T(128)} %get-tuple-element.804, bf16[512,2,128]{2,0,1:T(8,128)(2,1)S(1)} %get-tuple-element.829, f32[2,512,512]{1,2,0:T(8,128)S(1)} %get-tuple-element.731, f32[2,512]{1,0:T(2,128)S(1)} %get-tuple-element.733, ...), kind=kOutput, calls=%fused_computation.40.clone.1 | convolution fusion | flops 137101312 | bytes 3678720 | tf_op jit(solution)/shard_map/while/body/eval_jaxpr/kqc,ckd->qkd/dot_general | solution.py:64
  119.2 2.8 %fusion.119 = f32[8,512,2,128]{3,1,2,0:T(8,128)} fusion(f32[8,512,2,128]{3,1,2,0:T(8,128)} %get-tuple-element.807, s32[]{:T(128)} %get-tuple-element.804, bf16[512,2,128]{2,0,1:T(8,128)(2,1)S(1)} %get-tuple-element.829, f32[2,512,512]{1,2,0:T(8,128)S(1)} %get-tuple-element.731, f32[2,512]{1,0:T(2,128)S(1)} %get-tuple-element.733, ...), kind=kOutput, calls=%fused_computation.40.clone.1 | convolution fusion | flops 137101312 | bytes 3678720 | tf_op jit(solution)/shard_map/while/body/eval_jaxpr/kqc,ckd->qkd/dot_general | solution.py:64
  123.6 2.8 %fusion.119 = f32[8,512,2,128]{3,1,2,0:T(8,128)} fusion(f32[8,512,2,128]{3,1,2,0:T(8,128)} %get-tuple-element.807, s32[]{:T(128)} %get-tuple-element.804, bf16[512,2,128]{2,0,1:T(8,128)(2,1)S(1)} %get-tuple-element.829, f32[2,512,512]{1,2,0:T(8,128)S(1)} %get-tuple-element.731, f32[2,512]{1,0:T(2,128)S(1)} %get-tuple-element.733, ...), kind=kOutput, calls=%fused_computation.40.clone.1 | convolution fusion | flops 137101312 | bytes 3678720 | tf_op jit(solution)/shard_map/while/body/eval_jaxpr/kqc,ckd->qkd/dot_general | solution.py:64
  128.0 2.8 %fusion.119 = f32[8,512,2,128]{3,1,2,0:T(8,128)} fusion(f32[8,512,2,128]{3,1,2,0:T(8,128)} %get-tuple-element.807, s32[]{:T(128)} %get-tuple-element.804, bf16[512,2,128]{2,0,1:T(8,128)(2,1)S(1)} %get-tuple-element.829, f32[2,512,512]{1,2,0:T(8,128)S(1)} %get-tuple-element.731, f32[2,512]{1,0:T(2,128)S(1)} %get-tuple-element.733, ...), kind=kOutput, calls=%fused_computation.40.clone.1 | convolution fusion | flops 137101312 | bytes 3678720 | tf_op jit(solution)/shard_map/while/body/eval_jaxpr/kqc,ckd->qkd/dot_general | solution.py:64
  132.3 2.8 %fusion.119 = f32[8,512,2,128]{3,1,2,0:T(8,128)} fusion(f32[8,512,2,128]{3,1,2,0:T(8,128)} %get-tuple-element.807, s32[]{:T(128)} %get-tuple-element.804, bf16[512,2,128]{2,0,1:T(8,128)(2,1)S(1)} %get-tuple-element.829, f32[2,512,512]{1,2,0:T(8,128)S(1)} %get-tuple-element.731, f32[2,512]{1,0:T(2,128)S(1)} %get-tuple-element.733, ...), kind=kOutput, calls=%fused_computation.40.clone.1 | convolution fusion | flops 137101312 | bytes 3678720 | tf_op jit(solution)/shard_map/while/body/eval_jaxpr/kqc,ckd->qkd/dot_general | solution.py:64
  136.6 2.8 %fusion.119 = f32[8,512,2,128]{3,1,2,0:T(8,128)} fusion(f32[8,512,2,128]{3,1,2,0:T(8,128)} %get-tuple-element.807, s32[]{:T(128)} %get-tuple-element.804, bf16[512,2,128]{2,0,1:T(8,128)(2,1)S(1)} %get-tuple-element.829, f32[2,512,512]{1,2,0:T(8,128)S(1)} %get-tuple-element.731, f32[2,512]{1,0:T(2,128)S(1)} %get-tuple-element.733, ...), kind=kOutput, calls=%fused_computation.40.clone.1 | convolution fusion | flops 137101312 | bytes 3678720 | tf_op jit(solution)/shard_map/while/body/eval_jaxpr/kqc,ckd->qkd/dot_general | solution.py:64
  141.0 2.8 %fusion.119 = f32[8,512,2,128]{3,1,2,0:T(8,128)} fusion(f32[8,512,2,128]{3,1,2,0:T(8,128)} %get-tuple-element.807, s32[]{:T(128)} %get-tuple-element.804, bf16[512,2,128]{2,0,1:T(8,128)(2,1)S(1)} %get-tuple-element.829, f32[2,512,512]{1,2,0:T(8,128)S(1)} %get-tuple-element.731, f32[2,512]{1,0:T(2,128)S(1)} %get-tuple-element.733, ...), kind=kOutput, calls=%fused_computation.40.clone.1 | convolution fusion | flops 137101312 | bytes 3678720 | tf_op jit(solution)/shard_map/while/body/eval_jaxpr/kqc,ckd->qkd/dot_general | solution.py:64
  144.4 2.4 broadcast.125
  146.8 34.8 %while.45 = (s32[]{:T(128)}, f32[8,2,512]{2,1,0:T(2,128)S(1)}, f32[8,512,2,128]{3,1,2,0:T(8,128)}, f32[8,2,512]{2,1,0:T(2,128)S(1)}, f32[8,2,512]{2,1,0:T(2,128)...) while((s32[]{:T(128)}, f32[8,2,512]{2,1,0:T(2,128)S(1)}, ...), condition=%wide.region_15.16_spmd.clone, body=%wide.region_12.15_spmd.clone.sunk | while | flops 276566016 | bytes 9241753 | solution.py:73
  147.8 2.8 %fusion.127 = f32[8,512,2,128]{3,1,2,0:T(8,128)} fusion(f32[8,512,2,128]{3,1,2,0:T(8,128)} %get-tuple-element.853, s32[]{:T(128)} %get-tuple-element.851, bf16[512,2,128]{2,0,1:T(8,128)(2,1)S(1)} %get-tuple-element.874, f32[2,512,512]{1,2,0:T(8,128)S(1)} %get-tuple-element.751, f32[2,512]{1,0:T(2,128)S(1)} %get-tuple-element.753, ...), kind=kOutput, calls=%fused_computation.71.clone.1 | convolution fusion | flops 137101312 | bytes 3678720 | tf_op jit(solution)/shard_map/while/body/eval_jaxpr/kqc,ckd->qkd/dot_general | solution.py:64
  152.1 2.8 %fusion.127 = f32[8,512,2,128]{3,1,2,0:T(8,128)} fusion(f32[8,512,2,128]{3,1,2,0:T(8,128)} %get-tuple-element.853, s32[]{:T(128)} %get-tuple-element.851, bf16[512,2,128]{2,0,1:T(8,128)(2,1)S(1)} %get-tuple-element.874, f32[2,512,512]{1,2,0:T(8,128)S(1)} %get-tuple-element.751, f32[2,512]{1,0:T(2,128)S(1)} %get-tuple-element.753, ...), kind=kOutput, calls=%fused_computation.71.clone.1 | convolution fusion | flops 137101312 | bytes 3678720 | tf_op jit(solution)/shard_map/while/body/eval_jaxpr/kqc,ckd->qkd/dot_general | solution.py:64
  156.4 2.8 %fusion.127 = f32[8,512,2,128]{3,1,2,0:T(8,128)} fusion(f32[8,512,2,128]{3,1,2,0:T(8,128)} %get-tuple-element.853, s32[]{:T(128)} %get-tuple-element.851, bf16[512,2,128]{2,0,1:T(8,128)(2,1)S(1)} %get-tuple-element.874, f32[2,512,512]{1,2,0:T(8,128)S(1)} %get-tuple-element.751, f32[2,512]{1,0:T(2,128)S(1)} %get-tuple-element.753, ...), kind=kOutput, calls=%fused_computation.71.clone.1 | convolution fusion | flops 137101312 | bytes 3678720 | tf_op jit(solution)/shard_map/while/body/eval_jaxpr/kqc,ckd->qkd/dot_general | solution.py:64
  159.3 0.6 fusion.125
  160.8 2.8 %fusion.127 = f32[8,512,2,128]{3,1,2,0:T(8,128)} fusion(f32[8,512,2,128]{3,1,2,0:T(8,128)} %get-tuple-element.853, s32[]{:T(128)} %get-tuple-element.851, bf16[512,2,128]{2,0,1:T(8,128)(2,1)S(1)} %get-tuple-element.874, f32[2,512,512]{1,2,0:T(8,128)S(1)} %get-tuple-element.751, f32[2,512]{1,0:T(2,128)S(1)} %get-tuple-element.753, ...), kind=kOutput, calls=%fused_computation.71.clone.1 | convolution fusion | flops 137101312 | bytes 3678720 | tf_op jit(solution)/shard_map/while/body/eval_jaxpr/kqc,ckd->qkd/dot_general | solution.py:64
  165.1 2.8 %fusion.127 = f32[8,512,2,128]{3,1,2,0:T(8,128)} fusion(f32[8,512,2,128]{3,1,2,0:T(8,128)} %get-tuple-element.853, s32[]{:T(128)} %get-tuple-element.851, bf16[512,2,128]{2,0,1:T(8,128)(2,1)S(1)} %get-tuple-element.874, f32[2,512,512]{1,2,0:T(8,128)S(1)} %get-tuple-element.751, f32[2,512]{1,0:T(2,128)S(1)} %get-tuple-element.753, ...), kind=kOutput, calls=%fused_computation.71.clone.1 | convolution fusion | flops 137101312 | bytes 3678720 | tf_op jit(solution)/shard_map/while/body/eval_jaxpr/kqc,ckd->qkd/dot_general | solution.py:64
  168.0 0.6 fusion.125
  169.5 2.9 %fusion.127 = f32[8,512,2,128]{3,1,2,0:T(8,128)} fusion(f32[8,512,2,128]{3,1,2,0:T(8,128)} %get-tuple-element.853, s32[]{:T(128)} %get-tuple-element.851, bf16[512,2,128]{2,0,1:T(8,128)(2,1)S(1)} %get-tuple-element.874, f32[2,512,512]{1,2,0:T(8,128)S(1)} %get-tuple-element.751, f32[2,512]{1,0:T(2,128)S(1)} %get-tuple-element.753, ...), kind=kOutput, calls=%fused_computation.71.clone.1 | convolution fusion | flops 137101312 | bytes 3678720 | tf_op jit(solution)/shard_map/while/body/eval_jaxpr/kqc,ckd->qkd/dot_general | solution.py:64
  173.8 2.8 %fusion.127 = f32[8,512,2,128]{3,1,2,0:T(8,128)} fusion(f32[8,512,2,128]{3,1,2,0:T(8,128)} %get-tuple-element.853, s32[]{:T(128)} %get-tuple-element.851, bf16[512,2,128]{2,0,1:T(8,128)(2,1)S(1)} %get-tuple-element.874, f32[2,512,512]{1,2,0:T(8,128)S(1)} %get-tuple-element.751, f32[2,512]{1,0:T(2,128)S(1)} %get-tuple-element.753, ...), kind=kOutput, calls=%fused_computation.71.clone.1 | convolution fusion | flops 137101312 | bytes 3678720 | tf_op jit(solution)/shard_map/while/body/eval_jaxpr/kqc,ckd->qkd/dot_general | solution.py:64
  178.2 2.8 %fusion.127 = f32[8,512,2,128]{3,1,2,0:T(8,128)} fusion(f32[8,512,2,128]{3,1,2,0:T(8,128)} %get-tuple-element.853, s32[]{:T(128)} %get-tuple-element.851, bf16[512,2,128]{2,0,1:T(8,128)(2,1)S(1)} %get-tuple-element.874, f32[2,512,512]{1,2,0:T(8,128)S(1)} %get-tuple-element.751, f32[2,512]{1,0:T(2,128)S(1)} %get-tuple-element.753, ...), kind=kOutput, calls=%fused_computation.71.clone.1 | convolution fusion | flops 137101312 | bytes 3678720 | tf_op jit(solution)/shard_map/while/body/eval_jaxpr/kqc,ckd->qkd/dot_general | solution.py:64
  181.6 2.9 %fusion.73 = bf16[512,2,8,128]{3,0,1,2:T(8,128)(2,1)S(1)} fusion(f32[8,512,2,128]{3,1,2,0:T(8,128)} %get-tuple-element.167, f32[8,512,2]{1,2,0:T(2,128)S(1)} %bitcast.213), kind=kLoop, calls=%fused_computation.96 | loop fusion | flops 2097152 | bytes 6324224 | tf_op jit(solution)/shard_map/convert_element_type | solution.py:89
  184.5 2.7 %copy.75 = bf16[512,2,8,128]{3,2,1,0:T(8,128)(2,1)} copy(bf16[512,2,8,128]{3,0,1,2:T(8,128)(2,1)S(1)} %fusion.73) | data formatting | bytes 4194304 | tf_op jit(solution)/shard_map/convert_element_type | solution.py:89
  187.1 2.8 %convert_element_type.34 = bf16[4,128,2048]{2,1,0:T(8,128)(2,1)S(1)} reshape(bf16[512,2,8,128]{3,2,1,0:T(8,128)(2,1)} %copy.75) | data formatting | bytes 4194304 | tf_op jit(solution)/shard_map/convert_element_type | solution.py:89
  190.0 51.0 %all_to_all.64 = bf16[4,128,2048]{2,1,0:T(8,128)(2,1)} all-to-all(bf16[4,128,2048]{2,1,0:T(8,128)(2,1)S(1)} %convert_element_type.34), channel_id=1, replica_groups=mesh['head'=4,'outer'=2,'inner'=4] {'head'}, dimensions={0} | all-to-all | bytes 4194304 | tf_op jit(solution)/shard_map/all_to_all | solution.py:90
  241.0 3.0 %copy.76 = bf16[128,4,2048]{0,2,1:T(8,128)(2,1)S(1)} copy(bf16[128,4,2048]{2,0,1:T(8,128)(2,1)} %bitcast.202) | data formatting | bytes 4194304 | tf_op jit(solution)/shard_map/all_to_all | solution.py:90
  244.0 2.9 %copy.77 = bf16[128,8192]{1,0:T(8,128)(2,1)} copy(bf16[128,8192]{0,1:T(8,128)(2,1)S(1)} %bitcast.203) | data formatting | bytes 4194304 | tf_op jit(solution)/shard_map/all_to_all | solution.py:90
  (158 shorter events, 32.5 us)
Async XLA Ops:
  0.0 20.6 %copy-start = (bf16[128,8192]{1,0:T(8,128)(2,1)S(1)}, bf16[128,8192]{1,0:T(8,128)(2,1)}, u32[]{:S(2)}) copy-start(bf16[128,8192]{1,0:T(8,128)(2,1)} %param.10) | copy-start | bytes 6291460
  1.9 15.3 %all-to-all-start.1 = ((bf16[128,4,256]{0,2,1:T(8,128)(2,1)}), bf16[128,4,256]{0,2,1:T(8,128)(2,1)S(1)}, u32[]{:S(2)}, u32[]{:S(2)}) async-start(bf16[128,4,256]{0,2,1:T(8,128)(2,1)} %bitcast.2), calls=%async_computation.1 | async-start | bytes 524288 | tf_op jit(solution)/shard_map/all_to_all | solution.py:26
  17.2 10.4 %all-to-all-start.2 = ((bf16[128,4,256]{0,2,1:T(8,128)(2,1)}), bf16[128,4,256]{0,2,1:T(8,128)(2,1)S(1)}, u32[]{:S(2)}, u32[]{:S(2)}) async-start(bf16[128,4,256]{0,2,1:T(8,128)(2,1)} %bitcast.4), calls=%async_computation.2 | async-start | bytes 524288 | tf_op jit(solution)/shard_map/all_to_all | solution.py:27
  27.6 49.0 %all-to-all-start = ((bf16[128,4,2048]{2,0,1:T(8,128)(2,1)}), bf16[128,4,2048]{2,0,1:T(8,128)(2,1)S(1)}, u32[]{:S(2)}, u32[]{:S(2)}) async-start(bf16[128,4,2048]{2,0,1:T(8,128)(2,1)} %bitcast.143), calls=%async_computation | async-start | bytes 4194304 | tf_op jit(solution)/shard_map/all_to_all | solution.py:25
  31.2 17.2 %copy-start.3 = (s32[8]{0:T(128)S(1)}, s32[8]{0:T(128)}, u32[]{:S(2)}) copy-start(s32[8]{0:T(128)} %param.13) | copy-start | bytes 100
  31.6 11.6 %collective-permute-start = (bf16[2,512,256]{2,1,0:T(8,128)(2,1)S(1)}, bf16[2,512,256]{2,1,0:T(8,128)(2,1)}, u32[]{:S(2)}, u32[]{:S(2)}) collective-permute-start(bf16[2,512,256]{2,1,0:T(8,128)(2,1)S(1)} %pad_maximum_fusion), channel_id=1, source_target_pairs={{0,1},{1,2},{2,3},{3,4},{4,5},{5,6},{6,7},{8,9},{9,10},{10,11},{11... | collective-permute-start | bytes 1572872 | tf_op jit(solution)/shard_map/ppermute | solution.py:13
  43.2 13.9 %collective-permute-start.1 = (bf16[2,512,256]{2,1,0:T(8,128)(2,1)}, bf16[2,512,256]{2,1,0:T(8,128)(2,1)}, u32[]{:S(2)}, u32[]{:S(2)}) collective-permute-start(bf16[2,512,256]{2,1,0:T(8,128)(2,1)} %collective-permute-done), channel_id=1, source_target_pairs={{0,1},{1,2},{2,3},{3,4},{4,5},{5,6},{6,7},{8,9},{9,10},{10,11},{11... | collective-permute-start | bytes 1572872 | tf_op jit(solution)/shard_map/ppermute | solution.py:13
  80.5 1.0 copy-start.2
  83.8 1.0 copy-start.2
  87.2 1.0 copy-start.2
  90.5 1.0 copy-start.2
  93.9 1.0 copy-start.2
  97.2 1.0 copy-start.2
  100.6 1.0 copy-start.2
  103.9 1.0 copy-start.2
  107.2 2.4 copy-start.1
where the time goes:
time: 249 us; the launch traced here: 247 us
  matrix products  73 us (29%)
  blocking collectives  51 us (20%)
  waiting for transfers between devices  42.7 us (17%)
  local copies, waits for them, and re-layouts  30.7 us (12%)
  other arithmetic  25.2 us (10%)
  starting transfers between devices  22.9 us (9%)
    dot_general x24, matrix products, one_group(): jnp.einsum('kqc,ckd->qkd', weights.astype(jnp.bfloat16), value_heads, pre...  59.7 us
    all_to_all x1, blocking collectives, per_device(): lax.all_to_all(outcome, 'head', split_axis=0, concat_axis=1, tiled=True)  51 us
    all_to_all x1, waiting for transfers between devices, per_device(): lax.all_to_all(query, 'head', split_axis=1, concat_axis=0, tiled=True)  17.9 us
    reduce_sum x24, other arithmetic, one_group(): new_total = running_total * shrink + jnp.sum(weights, axis=2)  13.5 us
    dot_general x24, matrix products, one_group(): jnp.einsum('qkd,ckd->kqc', query_part, key_heads, preferred_element_type=...  13.3 us
    ppermute x2, waiting for transfers between devices, from_behind(): lax.ppermute(value, axis, [(source, source + steps) for source in range(l...  12.3 us
    ppermute x2, starting transfers between devices, from_behind(): lax.ppermute(value, axis, [(source, source + steps) for source in range(l...  9.49 us
    and x24, other arithmetic, attend(): (query_docs[:, None] == key_docs[None, :]) & (key_pos[None, :] <= query_p...  7.46 us
  transfers between devices with their start and end apart: 5, of which 5 were waited for; matrix products, arithmetic and copies ran while one was open for 4% of the time, Pallas kernels for 0%

commit v1 on v0

--- a/solution.py
+++ b/solution.py
@@ -22,7 +22,12 @@
 
 def per_device(query, keys, values, lengths):
     query_local, keys_local, values_local = (
-        lax.all_to_all(query, "head", split_axis=1, concat_axis=0, tiled=True),
+        jnp.concatenate(
+            lax.all_to_all(
+                jnp.stack(jnp.split(query, lax.axis_size("head"), axis=1)), "head", 0, 0
+            ),
+            axis=0,
+        ),
         lax.all_to_all(keys, "head", split_axis=1, concat_axis=0, tiled=True),
         lax.all_to_all(values, "head", split_axis=1, concat_axis=0, tiled=True),
     )

time: 249 us -> 248 us (level)
  local copies, waits for them, and re-layouts: 30.7 us -> 28.1 us
    another operation x8 -> x9, local copies, waits for them, and re-layouts: 7.23 us -> 7.37 us
where the time goes in v1:
time: 248 us; the launch traced here: 246 us
  matrix products  73 us (29%)
  blocking collectives  51.3 us (21%)
  waiting for transfers between devices  42.6 us (17%)
  local copies, waits for them, and re-layouts  28.1 us (11%)
  other arithmetic  26.8 us (11%)
  starting transfers between devices  22.9 us (9%)
    dot_general x24, matrix products, one_group(): jnp.einsum('kqc,ckd->qkd', weights.astype(jnp.bfloat16), value_heads, pre...  59.7 us
    all_to_all x1, blocking collectives, per_device(): lax.all_to_all(outcome, 'head', split_axis=0, concat_axis=1, tiled=True)  51.3 us
    all_to_all x1, waiting for transfers between devices, per_device(): lax.all_to_all(jnp.stack(jnp.split(query, lax.axis_size('head'), axis=1))...  17.9 us
    reduce_sum x24, other arithmetic, one_group(): new_total = running_total * shrink + jnp.sum(weights, axis=2)  13.6 us
    dot_general x24, matrix products, one_group(): jnp.einsum('qkd,ckd->kqc', query_part, key_heads, preferred_element_type=...  13.3 us
    ppermute x2, waiting for transfers between devices, from_behind(): lax.ppermute(value, axis, [(source, source + steps) for source in range(l...  12.3 us
    ppermute x2, starting transfers between devices, from_behind(): lax.ppermute(value, axis, [(source, source + steps) for source in range(l...  9.49 us
    and x24, other arithmetic, attend(): (query_docs[:, None] == key_docs[None, :]) & (key_pos[None, :] <= query_p...  7.46 us
  transfers between devices with their start and end apart: 5, of which 5 were waited for; matrix products, arithmetic and copies ran while one was open for 4% of the time, Pallas kernels for 0%

profile of v1, /device:TPU:0, one launch (start us, length us, event | category | flops | bytes accessed | tf_op | source)
XLA Modules:
  0.0 246.1 jit_solution(13038006075677905374)
XLA Ops:
  0.0 1.9 copy.53
  1.9 6.3 %all-to-all-start.1 = ((bf16[128,4,256]{0,2,1:T(8,128)(2,1)}), bf16[128,4,256]{0,2,1:T(8,128)(2,1)S(1)}, u32[]{:S(2)}, u32[]{:S(2)}) async-start(bf16[128,4,256]{0,2,1:T(8,128)(2,1)} %bitcast.5), calls=%async_computation.1 | async-start | bytes 524288 | tf_op jit(solution)/shard_map/all_to_all | solution.py:31
  8.3 1.8 copy.55
  10.1 7.1 %all-to-all-done.1 = bf16[128,4,256]{0,2,1:T(8,128)(2,1)S(1)} async-done(((bf16[128,4,256]{0,2,1:T(8,128)(2,1)}), bf16[128,4,256]{0,2,1:T(8,128)(2,1)S(1)}, u32[]{:S(2)}, u32[]{:S(2)}) %all-to-all-start.1) | async-done | bytes 262176 | tf_op jit(solution)/shard_map/all_to_all | solution.py:31
  17.2 3.4 %all-to-all-start.2 = ((bf16[128,4,256]{0,2,1:T(8,128)(2,1)}), bf16[128,4,256]{0,2,1:T(8,128)(2,1)S(1)}, u32[]{:S(2)}, u32[]{:S(2)}) async-start(bf16[128,4,256]{0,2,1:T(8,128)(2,1)} %bitcast.7), calls=%async_computation.2 | async-start | bytes 524288 | tf_op jit(solution)/shard_map/all_to_all | solution.py:32
  20.8 1.6 pad_maximum_fusion
  22.4 5.3 %all-to-all-done.2 = bf16[128,4,256]{0,2,1:T(8,128)(2,1)S(1)} async-done(((bf16[128,4,256]{0,2,1:T(8,128)(2,1)}), bf16[128,4,256]{0,2,1:T(8,128)(2,1)S(1)}, u32[]{:S(2)}, u32[]{:S(2)}) %all-to-all-start.2) | async-done | bytes 262176 | tf_op jit(solution)/shard_map/all_to_all | solution.py:32
  27.6 3.6 %all-to-all-start = ((bf16[4,128,2048]{2,1,0:T(8,128)(2,1)}), bf16[4,128,2048]{2,1,0:T(8,128)(2,1)S(1)}, u32[]{:S(2)}, u32[]{:S(2)}) async-start(bf16[4,128,2048]{2,1,0:T(8,128)(2,1)} %pad_maximum_fusion), calls=%async_computation | async-start | bytes 4194304 | tf_op jit(solution)/shard_map/all_to_all | solution.py:26
  31.6 4.2 %collective-permute-start = (bf16[2,512,256]{2,1,0:T(8,128)(2,1)S(1)}, bf16[2,512,256]{2,1,0:T(8,128)(2,1)}, u32[]{:S(2)}, u32[]{:S(2)}) collective-permute-start(bf16[2,512,256]{2,1,0:T(8,128)(2,1)S(1)} %pad_maximum_fusion.1), channel_id=1, source_target_pairs={{0,1},{1,2},{2,3},{3,4},{4,5},{5,6},{6,7},{8,9},{9,10},{10,11},{11... | collective-permute-start | bytes 1572872 | tf_op jit(solution)/shard_map/ppermute | solution.py:13
  35.8 7.3 %collective-permute-done = bf16[2,512,256]{2,1,0:T(8,128)(2,1)} collective-permute-done((bf16[2,512,256]{2,1,0:T(8,128)(2,1)S(1)}, bf16[2,512,256]{2,1,0:T(8,128)(2,1)}, u32[]{:S(2)}, u32[]{:S(2)}) %collective-permute-start) | collective-permute-done | bytes 524320 | tf_op jit(solution)/shard_map/ppermute | solution.py:13
  43.2 5.3 %collective-permute-start.1 = (bf16[2,512,256]{2,1,0:T(8,128)(2,1)}, bf16[2,512,256]{2,1,0:T(8,128)(2,1)}, u32[]{:S(2)}, u32[]{:S(2)}) collective-permute-start(bf16[2,512,256]{2,1,0:T(8,128)(2,1)} %collective-permute-done), channel_id=1, source_target_pairs={{0,1},{1,2},{2,3},{3,4},{4,5},{5,6},{6,7},{8,9},{9,10},{10,11},{11... | collective-permute-start | bytes 1572872 | tf_op jit(solution)/shard_map/ppermute | solution.py:13
  48.9 0.8 copy.59
  49.7 1.1 fusion.75
  51.2 0.8 copy.66
  52.1 5.0 %collective-permute-done.1 = bf16[2,512,256]{2,1,0:T(8,128)(2,1)} collective-permute-done((bf16[2,512,256]{2,1,0:T(8,128)(2,1)}, bf16[2,512,256]{2,1,0:T(8,128)(2,1)}, u32[]{:S(2)}, u32[]{:S(2)}) %collective-permute-start.1) | collective-permute-done | bytes 524320 | tf_op jit(solution)/shard_map/ppermute | solution.py:13
  57.1 1.1 fusion.74
  58.8 17.9 %all-to-all-done = bf16[4,128,2048]{2,1,0:T(8,128)(2,1)S(1)} async-done(((bf16[4,128,2048]{2,1,0:T(8,128)(2,1)}), bf16[4,128,2048]{2,1,0:T(8,128)(2,1)S(1)}, u32[]{:S(2)}, u32[]{:S(2)}) %all-to-all-start) | async-done | bytes 2097184 | tf_op jit(solution)/shard_map/all_to_all | solution.py:26
  76.7 0.6 copy.78
  77.8 2.4 broadcast.125.clone.1
  80.3 27.0 %while.43 = (s32[]{:T(128)}, f32[8,2,512]{2,1,0:T(2,128)S(1)}, f32[8,2,512]{2,1,0:T(2,128)S(1)}, f32[8,512,2,128]{3,1,2,0:T(8,128)}, bf16[8,512,2,128]{3,1,2,0:T...) while((s32[]{:T(128)}, f32[8,2,512]{2,1,0:T(2,128)S(1)}, ...), condition=%wide.region_5.6_spmd.clone, body=%wide.region_2.0_spmd.clone.sunk | while | flops 276435968 | bytes 9753745 | solution.py:78
  81.4 1.8 fusion.111
  83.2 0.6 fusion.109
  84.7 1.8 fusion.111
  86.6 0.6 fusion.109
  88.1 1.8 fusion.111
  91.5 1.8 fusion.111
  94.8 1.8 fusion.111
  98.2 1.8 fusion.111
  101.5 1.8 fusion.111
  104.8 1.8 fusion.111
  107.2 2.4 broadcast.125.clone
  109.6 34.8 %while.44 = (s32[]{:T(128)}, f32[8,2,512]{2,1,0:T(2,128)S(1)}, f32[8,2,512]{2,1,0:T(2,128)S(1)}, f32[8,512,2,128]{3,1,2,0:T(8,128)}, f32[8,2,512]{2,1,0:T(2,128)...) while((s32[]{:T(128)}, f32[8,2,512]{2,1,0:T(2,128)S(1)}, ...), condition=%wide.region_10.11_spmd.clone, body=%wide.region_7.10_spmd.clone.sunk | while | flops 276566016 | bytes 9245857 | solution.py:78
  110.6 2.8 %fusion.119 = f32[8,512,2,128]{3,1,2,0:T(8,128)} fusion(f32[8,512,2,128]{3,1,2,0:T(8,128)} %get-tuple-element.811, s32[]{:T(128)} %get-tuple-element.808, bf16[512,2,128]{2,0,1:T(8,128)(2,1)S(1)} %get-tuple-element.833, f32[2,512,512]{1,2,0:T(8,128)S(1)} %get-tuple-element.735, f32[2,512]{1,0:T(2,128)S(1)} %get-tuple-element.737, ...), kind=kOutput, calls=%fused_computation.40.clone.1 | convolution fusion | flops 137101312 | bytes 3678720 | tf_op jit(solution)/shard_map/while/body/eval_jaxpr/kqc,ckd->qkd/dot_general | solution.py:69
  114.9 2.8 %fusion.119 = f32[8,512,2,128]{3,1,2,0:T(8,128)} fusion(f32[8,512,2,128]{3,1,2,0:T(8,128)} %get-tuple-element.811, s32[]{:T(128)} %get-tuple-element.808, bf16[512,2,128]{2,0,1:T(8,128)(2,1)S(1)} %get-tuple-element.833, f32[2,512,512]{1,2,0:T(8,128)S(1)} %get-tuple-element.735, f32[2,512]{1,0:T(2,128)S(1)} %get-tuple-element.737, ...), kind=kOutput, calls=%fused_computation.40.clone.1 | convolution fusion | flops 137101312 | bytes 3678720 | tf_op jit(solution)/shard_map/while/body/eval_jaxpr/kqc,ckd->qkd/dot_general | solution.py:69
  119.2 2.8 %fusion.119 = f32[8,512,2,128]{3,1,2,0:T(8,128)} fusion(f32[8,512,2,128]{3,1,2,0:T(8,128)} %get-tuple-element.811, s32[]{:T(128)} %get-tuple-element.808, bf16[512,2,128]{2,0,1:T(8,128)(2,1)S(1)} %get-tuple-element.833, f32[2,512,512]{1,2,0:T(8,128)S(1)} %get-tuple-element.735, f32[2,512]{1,0:T(2,128)S(1)} %get-tuple-element.737, ...), kind=kOutput, calls=%fused_computation.40.clone.1 | convolution fusion | flops 137101312 | bytes 3678720 | tf_op jit(solution)/shard_map/while/body/eval_jaxpr/kqc,ckd->qkd/dot_general | solution.py:69
  123.6 2.8 %fusion.119 = f32[8,512,2,128]{3,1,2,0:T(8,128)} fusion(f32[8,512,2,128]{3,1,2,0:T(8,128)} %get-tuple-element.811, s32[]{:T(128)} %get-tuple-element.808, bf16[512,2,128]{2,0,1:T(8,128)(2,1)S(1)} %get-tuple-element.833, f32[2,512,512]{1,2,0:T(8,128)S(1)} %get-tuple-element.735, f32[2,512]{1,0:T(2,128)S(1)} %get-tuple-element.737, ...), kind=kOutput, calls=%fused_computation.40.clone.1 | convolution fusion | flops 137101312 | bytes 3678720 | tf_op jit(solution)/shard_map/while/body/eval_jaxpr/kqc,ckd->qkd/dot_general | solution.py:69
  127.9 2.8 %fusion.119 = f32[8,512,2,128]{3,1,2,0:T(8,128)} fusion(f32[8,512,2,128]{3,1,2,0:T(8,128)} %get-tuple-element.811, s32[]{:T(128)} %get-tuple-element.808, bf16[512,2,128]{2,0,1:T(8,128)(2,1)S(1)} %get-tuple-element.833, f32[2,512,512]{1,2,0:T(8,128)S(1)} %get-tuple-element.735, f32[2,512]{1,0:T(2,128)S(1)} %get-tuple-element.737, ...), kind=kOutput, calls=%fused_computation.40.clone.1 | convolution fusion | flops 137101312 | bytes 3678720 | tf_op jit(solution)/shard_map/while/body/eval_jaxpr/kqc,ckd->qkd/dot_general | solution.py:69
  132.3 2.8 %fusion.119 = f32[8,512,2,128]{3,1,2,0:T(8,128)} fusion(f32[8,512,2,128]{3,1,2,0:T(8,128)} %get-tuple-element.811, s32[]{:T(128)} %get-tuple-element.808, bf16[512,2,128]{2,0,1:T(8,128)(2,1)S(1)} %get-tuple-element.833, f32[2,512,512]{1,2,0:T(8,128)S(1)} %get-tuple-element.735, f32[2,512]{1,0:T(2,128)S(1)} %get-tuple-element.737, ...), kind=kOutput, calls=%fused_computation.40.clone.1 | convolution fusion | flops 137101312 | bytes 3678720 | tf_op jit(solution)/shard_map/while/body/eval_jaxpr/kqc,ckd->qkd/dot_general | solution.py:69
  136.6 2.8 %fusion.119 = f32[8,512,2,128]{3,1,2,0:T(8,128)} fusion(f32[8,512,2,128]{3,1,2,0:T(8,128)} %get-tuple-element.811, s32[]{:T(128)} %get-tuple-element.808, bf16[512,2,128]{2,0,1:T(8,128)(2,1)S(1)} %get-tuple-element.833, f32[2,512,512]{1,2,0:T(8,128)S(1)} %get-tuple-element.735, f32[2,512]{1,0:T(2,128)S(1)} %get-tuple-element.737, ...), kind=kOutput, calls=%fused_computation.40.clone.1 | convolution fusion | flops 137101312 | bytes 3678720 | tf_op jit(solution)/shard_map/while/body/eval_jaxpr/kqc,ckd->qkd/dot_general | solution.py:69
  141.0 2.8 %fusion.119 = f32[8,512,2,128]{3,1,2,0:T(8,128)} fusion(f32[8,512,2,128]{3,1,2,0:T(8,128)} %get-tuple-element.811, s32[]{:T(128)} %get-tuple-element.808, bf16[512,2,128]{2,0,1:T(8,128)(2,1)S(1)} %get-tuple-element.833, f32[2,512,512]{1,2,0:T(8,128)S(1)} %get-tuple-element.735, f32[2,512]{1,0:T(2,128)S(1)} %get-tuple-element.737, ...), kind=kOutput, calls=%fused_computation.40.clone.1 | convolution fusion | flops 137101312 | bytes 3678720 | tf_op jit(solution)/shard_map/while/body/eval_jaxpr/kqc,ckd->qkd/dot_general | solution.py:69
  144.4 2.4 broadcast.125
  146.8 34.8 %while.45 = (s32[]{:T(128)}, f32[8,2,512]{2,1,0:T(2,128)S(1)}, f32[8,512,2,128]{3,1,2,0:T(8,128)}, f32[8,2,512]{2,1,0:T(2,128)S(1)}, f32[8,2,512]{2,1,0:T(2,128)...) while((s32[]{:T(128)}, f32[8,2,512]{2,1,0:T(2,128)S(1)}, ...), condition=%wide.region_15.16_spmd.clone, body=%wide.region_12.15_spmd.clone.sunk | while | flops 276566016 | bytes 9241753 | solution.py:78
  147.7 2.8 %fusion.127 = f32[8,512,2,128]{3,1,2,0:T(8,128)} fusion(f32[8,512,2,128]{3,1,2,0:T(8,128)} %get-tuple-element.857, s32[]{:T(128)} %get-tuple-element.855, bf16[512,2,128]{2,0,1:T(8,128)(2,1)S(1)} %get-tuple-element.878, f32[2,512,512]{1,2,0:T(8,128)S(1)} %get-tuple-element.755, f32[2,512]{1,0:T(2,128)S(1)} %get-tuple-element.757, ...), kind=kOutput, calls=%fused_computation.71.clone.1 | convolution fusion | flops 137101312 | bytes 3678720 | tf_op jit(solution)/shard_map/while/body/eval_jaxpr/kqc,ckd->qkd/dot_general | solution.py:69
  150.6 0.6 fusion.125
  152.1 2.9 %fusion.127 = f32[8,512,2,128]{3,1,2,0:T(8,128)} fusion(f32[8,512,2,128]{3,1,2,0:T(8,128)} %get-tuple-element.857, s32[]{:T(128)} %get-tuple-element.855, bf16[512,2,128]{2,0,1:T(8,128)(2,1)S(1)} %get-tuple-element.878, f32[2,512,512]{1,2,0:T(8,128)S(1)} %get-tuple-element.755, f32[2,512]{1,0:T(2,128)S(1)} %get-tuple-element.757, ...), kind=kOutput, calls=%fused_computation.71.clone.1 | convolution fusion | flops 137101312 | bytes 3678720 | tf_op jit(solution)/shard_map/while/body/eval_jaxpr/kqc,ckd->qkd/dot_general | solution.py:69
  154.9 0.6 fusion.125
  156.4 2.8 %fusion.127 = f32[8,512,2,128]{3,1,2,0:T(8,128)} fusion(f32[8,512,2,128]{3,1,2,0:T(8,128)} %get-tuple-element.857, s32[]{:T(128)} %get-tuple-element.855, bf16[512,2,128]{2,0,1:T(8,128)(2,1)S(1)} %get-tuple-element.878, f32[2,512,512]{1,2,0:T(8,128)S(1)} %get-tuple-element.755, f32[2,512]{1,0:T(2,128)S(1)} %get-tuple-element.757, ...), kind=kOutput, calls=%fused_computation.71.clone.1 | convolution fusion | flops 137101312 | bytes 3678720 | tf_op jit(solution)/shard_map/while/body/eval_jaxpr/kqc,ckd->qkd/dot_general | solution.py:69
  159.3 0.6 fusion.125
  160.8 2.8 %fusion.127 = f32[8,512,2,128]{3,1,2,0:T(8,128)} fusion(f32[8,512,2,128]{3,1,2,0:T(8,128)} %get-tuple-element.857, s32[]{:T(128)} %get-tuple-element.855, bf16[512,2,128]{2,0,1:T(8,128)(2,1)S(1)} %get-tuple-element.878, f32[2,512,512]{1,2,0:T(8,128)S(1)} %get-tuple-element.755, f32[2,512]{1,0:T(2,128)S(1)} %get-tuple-element.757, ...), kind=kOutput, calls=%fused_computation.71.clone.1 | convolution fusion | flops 137101312 | bytes 3678720 | tf_op jit(solution)/shard_map/while/body/eval_jaxpr/kqc,ckd->qkd/dot_general | solution.py:69
  163.6 0.6 fusion.125
  165.1 2.8 %fusion.127 = f32[8,512,2,128]{3,1,2,0:T(8,128)} fusion(f32[8,512,2,128]{3,1,2,0:T(8,128)} %get-tuple-element.857, s32[]{:T(128)} %get-tuple-element.855, bf16[512,2,128]{2,0,1:T(8,128)(2,1)S(1)} %get-tuple-element.878, f32[2,512,512]{1,2,0:T(8,128)S(1)} %get-tuple-element.755, f32[2,512]{1,0:T(2,128)S(1)} %get-tuple-element.757, ...), kind=kOutput, calls=%fused_computation.71.clone.1 | convolution fusion | flops 137101312 | bytes 3678720 | tf_op jit(solution)/shard_map/while/body/eval_jaxpr/kqc,ckd->qkd/dot_general | solution.py:69
  168.0 0.6 fusion.125
  169.5 2.9 %fusion.127 = f32[8,512,2,128]{3,1,2,0:T(8,128)} fusion(f32[8,512,2,128]{3,1,2,0:T(8,128)} %get-tuple-element.857, s32[]{:T(128)} %get-tuple-element.855, bf16[512,2,128]{2,0,1:T(8,128)(2,1)S(1)} %get-tuple-element.878, f32[2,512,512]{1,2,0:T(8,128)S(1)} %get-tuple-element.755, f32[2,512]{1,0:T(2,128)S(1)} %get-tuple-element.757, ...), kind=kOutput, calls=%fused_computation.71.clone.1 | convolution fusion | flops 137101312 | bytes 3678720 | tf_op jit(solution)/shard_map/while/body/eval_jaxpr/kqc,ckd->qkd/dot_general | solution.py:69
  172.3 0.6 fusion.125
  173.9 2.8 %fusion.127 = f32[8,512,2,128]{3,1,2,0:T(8,128)} fusion(f32[8,512,2,128]{3,1,2,0:T(8,128)} %get-tuple-element.857, s32[]{:T(128)} %get-tuple-element.855, bf16[512,2,128]{2,0,1:T(8,128)(2,1)S(1)} %get-tuple-element.878, f32[2,512,512]{1,2,0:T(8,128)S(1)} %get-tuple-element.755, f32[2,512]{1,0:T(2,128)S(1)} %get-tuple-element.757, ...), kind=kOutput, calls=%fused_computation.71.clone.1 | convolution fusion | flops 137101312 | bytes 3678720 | tf_op jit(solution)/shard_map/while/body/eval_jaxpr/kqc,ckd->qkd/dot_general | solution.py:69
  176.7 0.6 fusion.125
  178.2 2.8 %fusion.127 = f32[8,512,2,128]{3,1,2,0:T(8,128)} fusion(f32[8,512,2,128]{3,1,2,0:T(8,128)} %get-tuple-element.857, s32[]{:T(128)} %get-tuple-element.855, bf16[512,2,128]{2,0,1:T(8,128)(2,1)S(1)} %get-tuple-element.878, f32[2,512,512]{1,2,0:T(8,128)S(1)} %get-tuple-element.755, f32[2,512]{1,0:T(2,128)S(1)} %get-tuple-element.757, ...), kind=kOutput, calls=%fused_computation.71.clone.1 | convolution fusion | flops 137101312 | bytes 3678720 | tf_op jit(solution)/shard_map/while/body/eval_jaxpr/kqc,ckd->qkd/dot_general | solution.py:69
  181.0 0.6 fusion.125
  181.6 2.9 %fusion.73 = bf16[512,2,8,128]{3,0,1,2:T(8,128)(2,1)S(1)} fusion(f32[8,512,2,128]{3,1,2,0:T(8,128)} %get-tuple-element.167, f32[8,512,2]{1,2,0:T(2,128)S(1)} %bitcast.215), kind=kLoop, calls=%fused_computation.96 | loop fusion | flops 2097152 | bytes 6324224 | tf_op jit(solution)/shard_map/convert_element_type | solution.py:94
  184.5 1.4 copy.72
  185.9 2.3 convert_element_type.34
  188.1 51.3 %all_to_all.53 = bf16[4,128,2048]{2,1,0:T(8,128)(2,1)S(1)} all-to-all(bf16[4,128,2048]{2,1,0:T(8,128)(2,1)} %convert_element_type.34), channel_id=1, replica_groups=mesh['head'=4,'outer'=2,'inner'=4] {'head'}, dimensions={0} | all-to-all | bytes 4194304 | tf_op jit(solution)/shard_map/all_to_all | solution.py:95
  239.5 2.5 %copy.73 = bf16[128,4,2048]{0,2,1:T(8,128)(2,1)} copy(bf16[128,4,2048]{2,0,1:T(8,128)(2,1)S(1)} %bitcast.205) | data formatting | bytes 4194304 | tf_op jit(solution)/shard_map/all_to_all | solution.py:95
  242.0 4.1 %copy.74 = bf16[128,8192]{1,0:T(8,128)(2,1)} copy(bf16[128,8192]{0,1:T(8,128)(2,1)} %bitcast.206) | data formatting | bytes 4194304 | tf_op jit(solution)/shard_map/all_to_all | solution.py:95
  (159 shorter events, 32.6 us)
Async XLA Ops:
  0.0 20.6 %copy-start = (bf16[128,8192]{1,0:T(8,128)(2,1)S(1)}, bf16[128,8192]{1,0:T(8,128)(2,1)}, u32[]{:S(2)}) copy-start(bf16[128,8192]{1,0:T(8,128)(2,1)} %param.10) | copy-start | bytes 6291460
  1.9 15.3 %all-to-all-start.1 = ((bf16[128,4,256]{0,2,1:T(8,128)(2,1)}), bf16[128,4,256]{0,2,1:T(8,128)(2,1)S(1)}, u32[]{:S(2)}, u32[]{:S(2)}) async-start(bf16[128,4,256]{0,2,1:T(8,128)(2,1)} %bitcast.5), calls=%async_computation.1 | async-start | bytes 524288 | tf_op jit(solution)/shard_map/all_to_all | solution.py:31
  17.2 10.4 %all-to-all-start.2 = ((bf16[128,4,256]{0,2,1:T(8,128)(2,1)}), bf16[128,4,256]{0,2,1:T(8,128)(2,1)S(1)}, u32[]{:S(2)}, u32[]{:S(2)}) async-start(bf16[128,4,256]{0,2,1:T(8,128)(2,1)} %bitcast.7), calls=%async_computation.2 | async-start | bytes 524288 | tf_op jit(solution)/shard_map/all_to_all | solution.py:32
  27.6 49.0 %all-to-all-start = ((bf16[4,128,2048]{2,1,0:T(8,128)(2,1)}), bf16[4,128,2048]{2,1,0:T(8,128)(2,1)S(1)}, u32[]{:S(2)}, u32[]{:S(2)}) async-start(bf16[4,128,2048]{2,1,0:T(8,128)(2,1)} %pad_maximum_fusion), calls=%async_computation | async-start | bytes 4194304 | tf_op jit(solution)/shard_map/all_to_all | solution.py:26
  31.2 17.2 %copy-start.3 = (s32[8]{0:T(128)S(1)}, s32[8]{0:T(128)}, u32[]{:S(2)}) copy-start(s32[8]{0:T(128)} %param.13) | copy-start | bytes 100
  31.6 11.6 %collective-permute-start = (bf16[2,512,256]{2,1,0:T(8,128)(2,1)S(1)}, bf16[2,512,256]{2,1,0:T(8,128)(2,1)}, u32[]{:S(2)}, u32[]{:S(2)}) collective-permute-start(bf16[2,512,256]{2,1,0:T(8,128)(2,1)S(1)} %pad_maximum_fusion.1), channel_id=1, source_target_pairs={{0,1},{1,2},{2,3},{3,4},{4,5},{5,6},{6,7},{8,9},{9,10},{10,11},{11... | collective-permute-start | bytes 1572872 | tf_op jit(solution)/shard_map/ppermute | solution.py:13
  43.2 13.9 %collective-permute-start.1 = (bf16[2,512,256]{2,1,0:T(8,128)(2,1)}, bf16[2,512,256]{2,1,0:T(8,128)(2,1)}, u32[]{:S(2)}, u32[]{:S(2)}) collective-permute-start(bf16[2,512,256]{2,1,0:T(8,128)(2,1)} %collective-permute-done), channel_id=1, source_target_pairs={{0,1},{1,2},{2,3},{3,4},{4,5},{5,6},{6,7},{8,9},{9,10},{10,11},{11... | collective-permute-start | bytes 1572872 | tf_op jit(solution)/shard_map/ppermute | solution.py:13
  80.5 1.0 copy-start.2
  83.8 1.0 copy-start.2
  87.2 1.0 copy-start.2
  90.5 1.0 copy-start.2
  93.9 1.0 copy-start.2
  97.2 1.0 copy-start.2
  100.6 1.0 copy-start.2
  103.9 1.0 copy-start.2
  107.2 2.4 copy-start.1
